TPU v7x, 128 devices: a whole 4x4x4 slice. The times are simulated.
128 devices in a mesh: rep: 8 (over z, y_hi), fsdp: 16 (over x, y_lo, core).
Axes of the slice: x: 4, y: 4 (y_hi: 2, y_lo: 2; y = y_hi * 2 + y_lo), z: 4, core: 2. Of those that a mesh axis runs over, the one named last changes fastest.
Arguments:
- activations: bfloat16 [8, 32768, 4096], P('rep', 'fsdp'), may hold values from -6 to 6
- cotangent: bfloat16 [8, 32768, 1024], P('rep', 'fsdp'), may hold values from -0.03125 to 0.03125
- momentum: float32 [8, 4096, 1024], P('rep', 'fsdp'), may hold values from -6 to 6
Outputs:
- momentum_next: float32 [8, 4096, 1024], P('rep', 'fsdp')
- update: float32 [4096, 1024], P('fsdp')
All inputs are finite; a program needn't handle non-finite values.
Results may differ from a plain program's by a relative error of at most 0.0021.
Values sent between devices are 32-bit elements; how exact they have to be, the bound alone decides.
A program may use at most 128 MiB of HBM per device.

v0:
```python
import jax
import jax.numpy as jnp
from jax import lax
from jax.sharding import PartitionSpec as P

CH = 64
BAND = 16


momentum_decay = 0.9


def copy_for_each(array, axis):
    copies = jnp.broadcast_to(array, (lax.axis_size(axis), *array.shape))
    return lax.all_to_all(copies, axis, split_axis=0, concat_axis=0, tiled=True)


def over_copies(array, axis):
    return copy_for_each(array, axis).sum(axis=0)


def basis_rows(size, keep):
    freq = jnp.arange(keep, dtype=jnp.float32)[:, None]
    point = jnp.arange(size, dtype=jnp.float32)[None, :]
    waves = jnp.cos(jnp.pi * (2.0 * point + 1.0) * freq / (2.0 * size))
    scales = jnp.where(freq == 0.0, jnp.sqrt(1.0 / size), jnp.sqrt(2.0 / size))
    return waves * scales


def bands_of(field, basis):
    rows, width = field.shape
    blocks = field.reshape(rows // CH, CH, width // CH, CH)
    return jnp.einsum("kn,anbm,lm->akbl", basis, blocks, basis, precision=lax.Precision.HIGHEST)


def term_maker(normed, part):
    return lax.dot_general(
        normed, part, (((0,), (0,)), ((), ())), preferred_element_type=jnp.float32
    )


def settle(grad, field, basis):
    accumulated = momentum_decay * field + grad
    bands = bands_of(accumulated, basis)
    count, _, wide, _ = bands.shape
    blocks = jnp.einsum("kn,akbl,lm->anbm", basis, bands, basis, precision=lax.Precision.HIGHEST)
    return (accumulated - blocks.reshape(count * CH, wide * CH), bands)


def body(activations, cotangent, momentum):
    values = activations[0].astype(jnp.float32)
    stat = jnp.mean(values * values, axis=-1, keepdims=True)
    normed = (values * lax.rsqrt(stat + 1e-05)).astype(jnp.bfloat16)
    targets = cotangent[0]
    field = momentum[0]
    basis = basis_rows(CH, BAND)
    grad = lax.psum_scatter(term_maker(normed, targets), "fsdp", scatter_dimension=0, tiled=True)
    cleared, bands = settle(grad, field, basis)
    count, _, wide, _ = bands.shape
    summed = over_copies(bands, "rep")
    blocks = jnp.einsum("kn,akbl,lm->anbm", basis, summed, basis, precision=lax.Precision.HIGHEST)
    update = blocks.reshape(count * CH, wide * CH)
    groups = lax.axis_size("rep")
    return (cleared[None], update / groups)


def solution(mesh):
    return jax.shard_map(
        body,
        mesh=mesh,
        in_specs=(P("rep", "fsdp", None), P("rep", "fsdp", None), P("rep", "fsdp", None)),
        out_specs=(P("rep", "fsdp", None), P("fsdp", None)),
        check_vma=False,
    )
```

profile of v0, /device:TPU:0, one launch (start us, length us, event | category | flops | bytes accessed | tf_op | source)
XLA Modules:
  0.0 273.9 jit_solution(14855466990724900406)
XLA Ops:
  7.2 7.5 %fusion = f32[2048]{0:T(1024)S(1)} fusion(bf16[1,2048,4096]{2,1,0:T(8,128)(2,1)} %param.3), kind=kLoop, calls=%fused_computation.2 | loop fusion | flops 25163776 | bytes 16785408 | tf_op jit(solution)/shard_map/reduce_sum | solution.py:52
  14.7 3.2 %copy-done = bf16[1,2048,4096]{2,1,0:T(8,128)(2,1)S(1)} copy-done((bf16[1,2048,4096]{2,1,0:T(8,128)(2,1)S(1)}, bf16[1,2048,4096]{2,1,0:T(8,128)(2,1)}, u32[]{:S(2)}) %copy-start) | copy-done | bytes 16777240
  17.9 23.4 %fusion.3 = f32[4096,1024]{1,0:T(8,128)} fusion(bf16[1,2048,4096]{2,1,0:T(8,128)(2,1)S(1)} %copy-done, f32[2048]{0:T(1024)S(1)} %add_rsqrt_fusion, bf16[1,2048,1024]{2,1,0:T(8,128)(2,1)} %param.4), kind=kOutput, calls=%fused_computation.5 | convolution fusion | flops 17205035008 | bytes 37756928 | tf_op jit(solution)/shard_map/dot_general | solution.py:37
  41.3 178.3 %reduce-scatter.2.cloned.1.call-done = f32[256,1024]{1,0:T(8,128)} async-done(((f32[4096,1024]{1,0:T(8,128)}), f32[256,1024]{1,0:T(8,128)}) %reduce-scatter.2.cloned.1.call-update) | async-done | bytes 1048592 | tf_op jit(solution)/shard_map/reduce_scatter | solution.py:57
  219.6 1.4 bitcast_add_fusion
  221.0 0.6 reshape.49
  221.6 1.7 fusion.7
  223.3 0.6 convolution_bitcast_fusion.1
  223.9 1.0 fusion.14
  225.1 2.4 broadcast_in_dim.20
  227.5 4.4 %reshape.52 = f32[8,1,16384]{2,1,0:T(1,128)} reshape(f32[8,4,16,16,16]{4,3,2,1,0:T(8,128)} %broadcast_in_dim.20) | data formatting | bytes 1048576
  231.9 7.6 %all-to-all-start = ((f32[8,1,16384]{2,1,0:T(1,128)}), f32[8,1,16384]{2,1,0:T(1,128)}, u32[]{:S(2)}, u32[]{:S(2)}) async-start(f32[8,1,16384]{2,1,0:T(1,128)} %reshape.52), calls=%async_computation.1 | async-start | bytes 1048576 | tf_op jit(solution)/shard_map/all_to_all | solution.py:15
  239.5 3.5 %convolution_bitcast_fusion = f32[4,64,16,64]{3,1,2,0:T(8,128)S(1)} fusion(f32[4,16,16,64]{3,2,1,0:T(8,128)S(1)} %fusion.14, f32[16]{0:T(128)S(1)} %compare_select_fusion, f32[64]{0:T(128)S(1)} %add_multiply_fusion), kind=kOutput, calls=%fused_computation.11 | convolution fusion | flops 50334720 | bytes 1311040 | tf_op jit(solution)/shard_map/kn,akbl,lm->anbm/dot_general | solution.py:46
  243.0 1.2 copy.12
  244.2 1.5 reshape.50
  245.7 2.3 subtract_bitcast_fusion
  248.1 2.1 all-to-all-done
  250.7 2.9 %reduce.1 = f32[8,16384]{1,0:T(8,128)S(1)} reduce(f32[8,1,16384]{2,1,0:T(1,128)} %all-to-all-done, f32[]{:T(128)} %broadcast.57), dimensions={1}, to_apply=%all_to_all.3.reduce_sub_computation | reduce | bytes 1048580 | tf_op jit(solution)/shard_map/all_to_all | solution.py:15
  253.6 3.3 %reshape.53 = f32[8,4,16,16,16]{4,3,2,1,0:T(8,128)} reshape(f32[8,16384]{1,0:T(8,128)S(1)} %reduce.1) | data formatting | bytes 1048576
  257.0 2.6 reduce_sum.19
  259.6 1.1 fusion.9
  260.6 3.7 %multiply_bitcast_fusion = f32[4,64,16,64]{3,1,2,0:T(8,128)S(1)} fusion(f32[4,16,16,64]{3,2,1,0:T(8,128)S(1)} %fusion.9, f32[16]{0:T(128)S(1)} %compare_select_fusion, f32[64]{0:T(128)S(1)} %add_multiply_fusion), kind=kOutput, calls=%fused_computation.10 | convolution fusion | flops 50596864 | bytes 1311040 | tf_op jit(solution)/shard_map/kn,akbl,lm->anbm/dot_general | solution.py:61
  264.3 1.2 copy.15
  265.6 1.5 div.39
  (10 shorter events, 0.8 us)
Async XLA Ops:
  7.2 212.5 %reduce-scatter.2.cloned.1.call-start = ((), (), s32[]{:S(2)}) async-start(), calls=%async_computation.2 | async-start | bytes 17825792 | tf_op jit(solution)/shard_map/reduce_scatter | solution.py:57
  7.2 10.7 %copy-start = (bf16[1,2048,4096]{2,1,0:T(8,128)(2,1)S(1)}, bf16[1,2048,4096]{2,1,0:T(8,128)(2,1)}, u32[]{:S(2)}) copy-start(bf16[1,2048,4096]{2,1,0:T(8,128)(2,1)} %param.3) | copy-start | bytes 50331652
  41.2 178.4 %copy-start.1 = (f32[1,256,1024]{2,1,0:T(8,128)S(1)}, f32[1,256,1024]{2,1,0:T(8,128)}, u32[]{:S(2)}) copy-start(f32[1,256,1024]{2,1,0:T(8,128)} %param.5) | copy-start | bytes 3145732
  231.9 18.3 %all-to-all-start = ((f32[8,1,16384]{2,1,0:T(1,128)}), f32[8,1,16384]{2,1,0:T(1,128)}, u32[]{:S(2)}, u32[]{:S(2)}) async-start(f32[8,1,16384]{2,1,0:T(1,128)} %reshape.52), calls=%async_computation.1 | async-start | bytes 1048576 | tf_op jit(solution)/shard_map/all_to_all | solution.py:15
Sparse Core Ops, SparseCore 0:
  41.4 178.1 reduce-scatter.1
where the time goes:
time: 277 us; the launch traced here: 274 us
  waiting for transfers between devices  180 us (65%)
  matrix products  35 us (13%)
  local copies, waits for them, and re-layouts  20 us (7%)
  other arithmetic  16.7 us (6%)
  between operations  14.1 us (5%)
  starting transfers between devices  7.6 us (3%)
    reduce_scatter x1, waiting for transfers between devices, body(): lax.psum_scatter(term_maker(normed, targets), 'fsdp', scatter_dimension=0...  178 us
    dot_general x1, matrix products, term_maker(): lax.dot_general(normed, part, (((0,), (0,)), ((), ())), preferred_element...  23.4 us
    unnamed x6, local copies, waits for them, and re-layouts  10.9 us
    all_to_all x1, starting transfers between devices, copy_for_each(): return lax.all_to_all(copies, axis, split_axis=0, concat_axis=0, tiled=True)  7.56 us
    reduce_sum x1, other arithmetic, body(): stat = jnp.mean(values * values, axis=-1, keepdims=True)  7.46 us
  transfers between devices with their start and end apart: 2, of which 2 were waited for; matrix products, arithmetic and copies ran while one was open for 3% of the time, Pallas kernels for 0%

commit v1 on v0

v1 whole, which is shorter than its diff:
```python
import functools

import jax
import jax.numpy as jnp
import numpy as np
from jax import lax
from jax.experimental import pallas as pl
from jax.experimental.pallas import tpu as pltpu
from jax.sharding import PartitionSpec as P

CH = 64
BAND = 16
momentum_decay = 0.9

TOK = 2048
D = 4096
KV = 1024
FB = 256
NA = 576
NB = KV - NA
HA, HB = NA // 2, NB // 2
HALF = KV // 2
RB = 128
XCH = 8
XR = TOK // XCH
MESH = pl.DeviceIdType.MESH
F32 = jnp.float32
BF16 = jnp.bfloat16
HI = lax.Precision.HIGHEST

OPP, NXP, NXM, OWN = 0, 2, 4, 6
NX = (NXP, NXM)
D2D = 0
XA = 8
XB = 20
YB = 26
YA = 30
RY = 31
RZ = 33
NSEM = 39
THROUGH, DIRECT, COMB = 0, 1, 2


def basis():
    freq = np.arange(BAND, dtype=np.float64)[:, None]
    point = np.arange(CH, dtype=np.float64)[None, :]
    waves = np.cos(np.pi * (2.0 * point + 1.0) * freq / (2.0 * CH))
    return (waves * np.where(freq == 0.0, np.sqrt(1.0 / CH), np.sqrt(2.0 / CH))).astype(np.float32)


def dot(a, b):
    return jnp.dot(a, b, precision=HI, preferred_element_type=F32)


def main_kernel(a_hbm, c_hbm, m_hbm, row_ref, rowt_ref, col_ref, colt_ref, next_ref, sum_ref,
                n, c, ct, m, buf, d2d, ra, rb, yb, ya, bsend, by, bsum, bz,
                send_sem, recv_sem, load_sem):
    rep = lax.axis_index("rep")
    me = lax.axis_index("fsdp")
    x, y, core = me // 4, (me // 2) % 2, me % 2
    z, yh = rep // 2, rep % 2
    partner = me + 1 - 2 * core
    xs = (((x + 1) % 4) * 4 + y * 2 + core, ((x + 3) % 4) * 4 + y * 2 + core)
    yp = x * 4 + (1 - y) * 2 + core
    rep_y = z * 2 + 1 - yh
    rep_z = [((z + i) % 4) * 2 + yh for i in (1, 2, 3)]

    barrier = pltpu.get_barrier_semaphore()
    for who in (partner, *xs, yp):
        pl.semaphore_signal(barrier, inc=1, device_id={"fsdp": who}, device_id_type=MESH)
    for who in (rep_y, *rep_z):
        pl.semaphore_signal(barrier, inc=1, device_id={"rep": who}, device_id_type=MESH)

    load_c = pltpu.make_async_copy(c_hbm, c, load_sem.at[0])
    load_c.start()

    def load_x(i):
        rows = pl.ds(pl.multiple_of(i * XR, XR), XR)
        return pltpu.make_async_copy(a_hbm.at[rows], n.at[rows], load_sem.at[2 + i])

    for i in range(XCH):
        load_x(i).start()
    load_m = pltpu.make_async_copy(m_hbm, m, load_sem.at[1])
    load_m.start()

    load_c.wait()

    @pl.loop(0, TOK // 256)
    def _(i):
        cols = pl.ds(pl.multiple_of(i * 256, 256), 256)
        ct[:, cols] = c[cols, :].T

    @pl.loop(0, XCH)
    def _(i):
        load_x(i).wait()

        @pl.loop(0, XR // RB)
        def _(j):
            rows = pl.ds(pl.multiple_of(i * XR + j * RB, RB), RB)
            squares = jnp.zeros((RB, 128), F32)
            for k in range(D // 128):
                v = n[rows, 128 * k : 128 * k + 128].astype(F32)
                squares = squares + v * v
            stat = jnp.sum(squares, axis=-1, keepdims=True) * (1.0 / D)
            scale = jnp.broadcast_to(lax.rsqrt(stat + 1e-05), (RB, 128))
            for k in range(D // 128):
                v = n[rows, 128 * k : 128 * k + 128].astype(F32)
                n[rows, 128 * k : 128 * k + 128] = (v * scale).astype(BF16)

    pl.semaphore_wait(barrier, 8)

    def remote(src, dst, sem, **where):
        return pltpu.make_async_remote_copy(
            src_ref=src, dst_ref=dst, send_sem=send_sem.at[sem], recv_sem=recv_sem.at[sem],
            device_id=where, device_id_type=MESH)

    def pair(k):
        return remote(buf.at[0, k], d2d.at[k], D2D + k, fsdp=partner)

    def half_a(s):
        return pl.ds(s * HA, HA)

    def half_b(s):
        return pl.ds(NA + s * HB, HB)

    def xa(s, j, kind):
        slot = (OPP if kind == THROUGH else NX[s]) + j
        rows = half_a(1 - s if kind == DIRECT else s)
        return remote(buf.at[1, slot, rows], ra.at[s, j, kind], XA + 6 * s + 3 * j + kind, fsdp=xs[s])

    def xb(s, kind):
        slot = (OPP if kind == THROUGH else NX[s]) + 1
        rows = half_b(1 - s if kind == DIRECT else s)
        return remote(buf.at[1, slot, rows], rb.at[s, kind], XB + 3 * s + kind, fsdp=xs[s])

    def yb_msg(i):
        return remote(buf.at[1, 2 * i, pl.ds(NA, NB)], yb.at[i], YB + i, fsdp=yp)

    def ya_msg():
        return remote(buf.at[1, OWN, pl.ds(0, NA)], ya, YA, fsdp=yp)

    def add(slot, rows, got):
        buf[1, slot, rows, :] = buf[1, slot, rows, :] + got[...]

    def take_xa(s, j, kind):
        xa(s, j, kind).wait_recv()
        slot = (NX[s] if kind == THROUGH else OWN) + j
        add(slot, half_a(1 - s if kind == DIRECT else s), ra.at[s, j, kind])

    def take_xb(s, kind):
        xb(s, kind).wait_recv()
        slot = (NX[s] if kind == THROUGH else OWN) + 1
        add(slot, half_b(1 - s if kind == DIRECT else s), rb.at[s, kind])

    def take_yb(i):
        yb_msg(i).wait_recv()
        add(2 * i + 1, pl.ds(NA, NB), yb.at[i])

    def comb_a(j):
        for s in (0, 1):
            take_xa(s, j, THROUGH)
            xa(s, j, COMB).start()

    @pl.loop(0, 17)
    def _(t):
        k, s = t // 2, t % 2

        @pl.when(t < 16)
        def _():
            i, j = k // 2, k % 2
            to_x = (x + 2 - i + 3 * (i // 2) + 2 * (i // 3)) % 4
            to_y = (y + 1 + j) % 2
            to_core = (core + 1 + s) % 2
            first = pl.multiple_of((to_x * 4 + to_y * 2 + to_core) * FB, FB)
            buf[s, k] = jnp.dot(ct[...], n[:, pl.ds(first, FB)], preferred_element_type=F32)

        @pl.when(jnp.logical_and(t < 16, s == 0))
        def _():
            pair(k).start()

        @pl.when(jnp.logical_and(t > 1, s == 0))
        def _():
            done = k - 1
            pair(done).wait_recv()

            @pl.loop(0, KV // 128)
            def _(i):
                rows = pl.ds(pl.multiple_of(i * 128, 128), 128)
                buf[1, done, rows, :] = buf[1, done, rows, :] + d2d[done, rows, :]

            @pl.when(done == 0)
            def _():
                for s in (0, 1):
                    xa(s, 0, THROUGH).start()
                yb_msg(0).start()

            @pl.when(done == 1)
            def _():
                for s in (0, 1):
                    xa(s, 1, THROUGH).start()

            @pl.when(done == 2)
            def _():
                xa(0, 0, DIRECT).start()
                yb_msg(1).start()

            @pl.when(done == 4)
            def _():
                xa(1, 0, DIRECT).start()
                yb_msg(2).start()
                comb_a(0)

            @pl.when(done == 5)
            def _():
                for s in (0, 1):
                    xa(s, 1, DIRECT).start()
                comb_a(1)
                take_yb(0)
                for s in (0, 1):
                    xb(s, THROUGH).start()

    take_yb(1)
    xb(0, DIRECT).start()
    for s in (0, 1):
        take_xa(s, 0, DIRECT)
    for s in (0, 1):
        take_xa(s, 0, COMB)
    ya_msg().start()
    yb_msg(3).start()
    take_yb(2)
    xb(1, DIRECT).start()
    for s in (0, 1):
        take_xa(s, 1, DIRECT)
    for s in (0, 1):
        take_xa(s, 1, COMB)

    load_m.wait()

    def to_y_rep(h):
        return remote(bsend.at[h], by.at[h], RY + h, rep=rep_y)

    def to_z_rep(h, i):
        return remote(bsum.at[h], bz.at[h, i], RZ + 3 * h + i, rep=rep_z[i])

    def finish(h):
        cols = slice(HALF * h, HALF * (h + 1))
        acc = momentum_decay * m[:, cols] + buf[1, OWN + 1, cols, :].T
        next_ref[:, cols] = acc
        bsend[h] = dot(dot(row_ref[...], acc), col_ref[...])
        to_y_rep(h).start()

    def clear(h):
        cols = slice(HALF * h, HALF * (h + 1))
        low = dot(dot(rowt_ref[...], bsend[h]), colt_ref[...])
        next_ref[:, cols] = next_ref[:, cols] - low

    def rep_y_take(h):
        to_y_rep(h).wait_recv()
        bsum[h] = bsend[h] + by[h]
        for i in range(3):
            to_z_rep(h, i).start()

    def rep_z_take(h):
        for i in range(3):
            to_z_rep(h, i).wait_recv()
        sum_ref[:, 128 * h : 128 * (h + 1)] = (bsum[h] + bz[h, 1]) + (bz[h, 0] + bz[h, 2])

    for s in (0, 1):
        take_xb(s, THROUGH)
        xb(s, COMB).start()
    ya_msg().wait_recv()
    add(OWN + 1, pl.ds(0, NA), ya)
    finish(0)
    clear(0)
    rep_y_take(0)
    for s in (0, 1):
        take_xb(s, DIRECT)
    take_yb(3)
    rep_z_take(0)
    for s in (0, 1):
        take_xb(s, COMB)
    finish(1)
    clear(1)
    rep_y_take(1)
    rep_z_take(1)

    for k in range(8):
        pair(k).wait_send()
    for s in (0, 1):
        for kind in range(3):
            for j in (0, 1):
                xa(s, j, kind).wait_send()
            xb(s, kind).wait_send()
    for i in range(4):
        yb_msg(i).wait_send()
    ya_msg().wait_send()
    for h in (0, 1):
        to_y_rep(h).wait_send()
        for i in range(3):
            to_z_rep(h, i).wait_send()


def out_kernel(next_in, sum_ref, rowt_ref, colt_ref, next_out, update_ref):
    next_out[...] = next_in[...]
    for h in (0, 1):
        part = sum_ref[:, 128 * h : 128 * (h + 1)] * 0.125
        update_ref[:, HALF * h : HALF * (h + 1)] = dot(dot(rowt_ref[...], part), colt_ref[...])


def vmem():
    return pl.BlockSpec(memory_space=pltpu.VMEM)


def body(activations, cotangent, momentum):
    base = basis()
    row = np.kron(np.eye(FB // CH, dtype=np.float32), base)
    colt = np.kron(np.eye(HALF // CH, dtype=np.float32), base)
    row, rowt = jnp.asarray(row), jnp.asarray(np.ascontiguousarray(row.T))
    colt, col = jnp.asarray(colt), jnp.asarray(np.ascontiguousarray(colt.T))
    any_space = pl.BlockSpec(memory_space=pl.ANY)
    nb = 4 * BAND
    cleared, summed = pl.pallas_call(
        main_kernel,
        name="step",
        out_shape=(jax.ShapeDtypeStruct((FB, KV), F32), jax.ShapeDtypeStruct((nb, 256), F32)),
        in_specs=[any_space] * 3 + [vmem()] * 4,
        out_specs=(vmem(), vmem()),
        scratch_shapes=[
            pltpu.VMEM((TOK, D), BF16),
            pltpu.VMEM((TOK, KV), BF16),
            pltpu.VMEM((KV, TOK), BF16),
            pltpu.VMEM((FB, KV), F32),
            pltpu.VMEM((2, 8, KV, FB), F32),
            pltpu.VMEM((8, KV, FB), F32),
            pltpu.VMEM((2, 2, 3, HA, FB), F32),
            pltpu.VMEM((2, 3, HB, FB), F32),
            pltpu.VMEM((4, NB, FB), F32),
            pltpu.VMEM((NA, FB), F32),
            pltpu.VMEM((2, nb, 128), F32),
            pltpu.VMEM((2, nb, 128), F32),
            pltpu.VMEM((2, nb, 128), F32),
            pltpu.VMEM((2, 3, nb, 128), F32),
            pltpu.SemaphoreType.DMA((NSEM,)),
            pltpu.SemaphoreType.DMA((NSEM,)),
            pltpu.SemaphoreType.DMA((2 + XCH,)),
        ],
        compiler_params=pltpu.CompilerParams(
            collective_id=0, has_side_effects=True, vmem_limit_bytes=64 * 1024 * 1024 - 256 * 1024),
    )(activations[0], cotangent[0], momentum[0], row, rowt, col, colt)
    cleared, update = pl.pallas_call(
        out_kernel,
        name="outputs",
        out_shape=(jax.ShapeDtypeStruct((FB, KV), F32), jax.ShapeDtypeStruct((FB, KV), F32)),
        in_specs=[vmem()] * 4,
        out_specs=(vmem(), vmem()),
    )(cleared, summed, rowt, colt)
    return cleared[None], update


def solution(mesh):
    return jax.shard_map(
        body,
        mesh=mesh,
        in_specs=(P("rep", "fsdp", None), P("rep", "fsdp", None), P("rep", "fsdp", None)),
        out_specs=(P("rep", "fsdp", None), P("fsdp", None)),
        check_vma=False,
    )
```

time: 277 us -> 93.7 us (0.34); the launches traced: 274 us -> 93.5 us
  waiting for transfers between devices: 180 us -> 0 us
  Pallas kernels: 0 us -> 92.9 us
  matrix products: 35 us -> 0 us
  local copies, waits for them, and re-layouts: 20 us -> 0 us
  other arithmetic: 16.7 us -> 0 us
  between operations: 14.1 us -> 0.64 us
  starting transfers between devices: 7.6 us -> 0 us
    reduce_scatter x1 -> x0, waiting for transfers between devices: 178 us -> none  [body(): lax.psum_scatter(term_maker(normed, targets), 'fsdp', scatter_dimension=0...]
    pallas_call x0 -> x2, Pallas kernels: none -> 92.9 us  [the longest x1 88.7 us: body(): pl.pallas_call(main_kernel, name='step', out_shape=(jax.ShapeDtypeStruct(...]
    dot_general x7 -> x0, matrix products: 35 us -> none  [the longest x1 23.4 us: term_maker(): lax.dot_general(normed, part, (((0,), (0,)), ((), ())), preferred_element...]
    unnamed x6 -> x0, local copies, waits for them, and re-layouts: 10.9 us -> none
    reduce_sum x2 -> x0, other arithmetic: 10 us -> none  [the longest x1 7.46 us: body(): stat = jnp.mean(values * values, axis=-1, keepdims=True)]
    all_to_all x1 -> x0, starting transfers between devices: 7.56 us -> none  [copy_for_each(): return lax.all_to_all(copies, axis, split_axis=0, concat_axis=0, tiled=True)]
    all_to_all x1 -> x0, other arithmetic: 2.93 us -> none  [copy_for_each(): return lax.all_to_all(copies, axis, split_axis=0, concat_axis=0, tiled=True)]
  transfers between devices with their start and end apart: 2 -> 0, of which waited for: 2 -> 0; matrix products, arithmetic and copies ran while one was open for 3% -> 0% of each run, Pallas kernels for 0% -> 0%
where the time goes in v1:
time: 93.7 us; the launch traced here: 93.5 us
  Pallas kernels  92.9 us (99%)
    pallas_call x1, Pallas kernels, body(): pl.pallas_call(main_kernel, name='step', out_shape=(jax.ShapeDtypeStruct(...  88.7 us
    pallas_call x1, Pallas kernels, body(): pl.pallas_call(out_kernel, name='outputs', out_shape=(jax.ShapeDtypeStruc...  4.22 us

profile of v1, /device:TPU:0, one launch (start us, length us, event | category | flops | bytes accessed | tf_op | source)
XLA Modules:
  0.0 93.5 jit_solution(2982962706552888106)
XLA Ops:
  0.6 88.7 %step.1 = (f32[256,1024]{1,0:T(8,128)}, f32[64,256]{1,0:T(8,128)}) custom-call(bf16[2048,4096]{1,0:T(8,128)(2,1)} %bitcast.4, bf16[2048,1024]{1,0:T(8,128)(2,1)} %bitcast.5, f32[256,1024]{1,0:T(8,128)} %bitcast.6, f32[64,256]{1,0:T(8,128)} %constant.8.clone.row_ref, f32[256,64]{1,0:T(8,128)} %constant.9.clone.rowt_ref, f32[512,128]{1,0:T(8,128)} %constant.11.clone.col_ref, ...), custom_call_target="tpu_custom_call" | custom-call | tf_op jit(solution)/shard_map/step/pallas_call | solution.py:322
  89.3 4.2 %outputs.1 = (f32[256,1024]{1,0:T(8,128)}, f32[256,1024]{1,0:T(8,128)}) custom-call(f32[256,1024]{1,0:T(8,128)} %get-tuple-element.6.next_in, f32[64,256]{1,0:T(8,128)} %get-tuple-element.7.sum_ref, f32[256,64]{1,0:T(8,128)} %constant.9.clone.rowt_ref, f32[128,512]{1,0:T(8,128)} %constant.10.clone.colt_ref), custom_call_target="tpu_custom_call" | custom-call | tf_op jit(solution)/shard_map/outputs/pallas_call | solution.py:350

commit v2 on v1

v2 whole, which is shorter than its diff:
```python
import functools

import jax
import jax.numpy as jnp
import numpy as np
from jax import lax
from jax.experimental import pallas as pl
from jax.experimental.pallas import tpu as pltpu
from jax.sharding import PartitionSpec as P

CH = 64
BAND = 16
momentum_decay = 0.9

TOK = 2048
D = 4096
KV = 1024
FB = 256
LOW = KV * BAND // CH
NA = (LOW, 320)
A0 = (0, LOW)
B0 = LOW + NA[1]
NB = KV - B0
HB = NB // 2
XCH = 8
XR = TOK // XCH
RB = 128
MESH = pl.DeviceIdType.MESH
F32 = jnp.float32
BF16 = jnp.bfloat16
HI = lax.Precision.HIGHEST

OWN = 6
D2D = 0
XA = 8
XB = 32
YB = 38
YA = 42
RY = 44
RZ = 45
NSEM = 48
THROUGH, DIRECT, COMB = 0, 1, 2


def basis():
    freq = np.arange(CH, dtype=np.float64)[:, None]
    point = np.arange(CH, dtype=np.float64)[None, :]
    waves = np.cos(np.pi * (2.0 * point + 1.0) * freq / (2.0 * CH))
    return waves * np.where(freq == 0.0, np.sqrt(1.0 / CH), np.sqrt(2.0 / CH))


def dot(a, b):
    return jnp.dot(a, b, precision=HI, preferred_element_type=F32)


def main_kernel(a_hbm, c_hbm, m_hbm, wave_ref, low_ref, lowt_ref, high_ref, next_ref, update_ref,
                n, c, ct, m, buf, d2d, ral, rah, rb, yb, yal, yah, mband, glow, bsend, by, bsum, bz,
                send_sem, recv_sem, load_sem):
    rep = lax.axis_index("rep")
    me = lax.axis_index("fsdp")
    x, y, core = me // 4, (me // 2) % 2, me % 2
    z, yh = rep // 2, rep % 2
    partner = me + 1 - 2 * core
    xs = (((x + 1) % 4) * 4 + y * 2 + core, ((x + 3) % 4) * 4 + y * 2 + core)
    yp = x * 4 + (1 - y) * 2 + core
    rep_y = z * 2 + 1 - yh
    rep_z = [((z + i) % 4) * 2 + yh for i in (1, 2, 3)]

    barrier = pltpu.get_barrier_semaphore()
    for who in (partner, *xs, yp):
        pl.semaphore_signal(barrier, inc=1, device_id={"fsdp": who}, device_id_type=MESH)
    for who in (rep_y, *rep_z):
        pl.semaphore_signal(barrier, inc=1, device_id={"rep": who}, device_id_type=MESH)

    load_c = pltpu.make_async_copy(c_hbm, c, load_sem.at[0])
    load_c.start()

    def load_x(i):
        rows = pl.ds(pl.multiple_of(i * XR, XR), XR)
        return pltpu.make_async_copy(a_hbm.at[rows], n.at[rows], load_sem.at[2 + i])

    for i in range(XCH):
        load_x(i).start()
    load_m = pltpu.make_async_copy(m_hbm, m, load_sem.at[1])
    load_m.start()
    load_c.wait()

    @pl.loop(0, XCH)
    def _(i):
        load_x(i).wait()
        tokens = pl.ds(pl.multiple_of(i * XR, XR), XR)
        for g in range(KV // 256):
            part = c[tokens, 256 * g : 256 * g + 256]
            wave = lax.dot_general(wave_ref[0], part, (((1,), (1,)), ((), ())), preferred_element_type=F32)
            wave = wave + lax.dot_general(wave_ref[1], part, (((1,), (1,)), ((), ())), preferred_element_type=F32)
            wave = wave.astype(BF16)
            ct[64 * g : 64 * g + 64, tokens] = wave[:64]
            ct[LOW + 192 * g : LOW + 192 * g + 192, tokens] = wave[64:]
        for j in range(XR // RB):
            rows = pl.ds(pl.multiple_of(i * XR + j * RB, RB), RB)
            squares = jnp.zeros((RB, 128), F32)
            for k in range(D // 128):
                v = n[rows, 128 * k : 128 * k + 128].astype(F32)
                squares = squares + v * v
            stat = jnp.sum(squares, axis=-1, keepdims=True) * (1.0 / D)
            scale = jnp.broadcast_to(lax.rsqrt(stat + 1e-05), (RB, 128))
            for k in range(D // 128):
                v = n[rows, 128 * k : 128 * k + 128].astype(F32)
                n[rows, 128 * k : 128 * k + 128] = (v * scale).astype(BF16)

    pl.semaphore_wait(barrier, 8)

    def remote(src, dst, sem, **where):
        return pltpu.make_async_remote_copy(
            src_ref=src, dst_ref=dst, send_sem=send_sem.at[sem], recv_sem=recv_sem.at[sem],
            device_id=where, device_id_type=MESH)

    def pair(k):
        return remote(buf.at[0, k], d2d.at[k], D2D + k, fsdp=partner)

    ra = (ral, rah)
    ya = (yal, yah)

    def half_a(p, s):
        return pl.ds(A0[p] + s * (NA[p] // 2), NA[p] // 2)

    def half_b(s):
        return pl.ds(B0 + s * HB, HB)

    def xa(p, s, j, kind):
        slot = 3 * j + (0 if kind == THROUGH else 1 + s)
        rows = half_a(p, 1 - s if kind == DIRECT else s)
        return remote(buf.at[1, slot, rows], ra[p].at[s, j, kind], XA + 12 * p + 6 * s + 3 * j + kind, fsdp=xs[s])

    def xb(s, kind):
        slot = 3 + (0 if kind == THROUGH else 1 + s)
        rows = half_b(1 - s if kind == DIRECT else s)
        return remote(buf.at[1, slot, rows], rb.at[s, kind], XB + 3 * s + kind, fsdp=xs[s])

    def yb_msg(i):
        return remote(buf.at[1, i if i < 3 else OWN, pl.ds(B0, NB)], yb.at[i], YB + i, fsdp=yp)

    def ya_msg(p):
        return remote(buf.at[1, OWN, pl.ds(A0[p], NA[p])], ya[p], YA + p, fsdp=yp)

    def add(slot, rows, got):
        buf[1, slot, rows, :] = buf[1, slot, rows, :] + got[...]

    def start_xa(p, j, kind):
        for s in (0, 1):
            xa(p, s, j, kind).start()

    def take_xa(p, j, kind):
        for s in (0, 1):
            xa(p, s, j, kind).wait_recv()
            slot = 3 * j + 1 + s if kind == THROUGH else OWN + j
            add(slot, half_a(p, 1 - s if kind == DIRECT else s), ra[p].at[s, j, kind])

    def comb_a(p, j):
        take_xa(p, j, THROUGH)
        start_xa(p, j, COMB)

    def take_xb(s, kind):
        xb(s, kind).wait_recv()
        slot = 3 + 1 + s if kind == THROUGH else OWN + 1
        add(slot, half_b(1 - s if kind == DIRECT else s), rb.at[s, kind])

    def take_yb(i):
        yb_msg(i).wait_recv()
        add(3 + i if i < 3 else OWN + 1, pl.ds(B0, NB), yb.at[i])

    def take_ya(p):
        ya_msg(p).wait_recv()
        add(OWN + 1, pl.ds(A0[p], NA[p]), ya[p])

    @pl.loop(0, 17)
    def _(t):
        k, s = t // 2, t % 2

        @pl.when(t < 16)
        def _():
            own = k // 6
            i = (1 - own) * (k % 3) + 3 * own
            j = (1 - own) * (k // 3) + own * (k - 6)
            to_x = (x + 2 - i + 3 * (i // 2) + 2 * (i // 3)) % 4
            to_y = (y + 1 + j) % 2
            to_core = (core + 1 + s) % 2
            first = pl.multiple_of((to_x * 4 + to_y * 2 + to_core) * FB, FB)
            buf[s, k] = jnp.dot(ct[...], n[:, pl.ds(first, FB)], preferred_element_type=F32)

        @pl.when(jnp.logical_and(t < 16, s == 0))
        def _():
            pair(k).start()

        @pl.when(jnp.logical_and(t > 1, s == 0))
        def _():
            done = k - 1
            pair(done).wait_recv()

            @pl.loop(0, KV // 128)
            def _(i):
                rows = pl.ds(pl.multiple_of(i * 128, 128), 128)
                buf[1, done, rows, :] = buf[1, done, rows, :] + d2d[done, rows, :]

            @pl.when(done == 0)
            def _():
                start_xa(0, 0, THROUGH)
                yb_msg(0).start()
                start_xa(1, 0, THROUGH)

            @pl.when(done == 1)
            def _():
                xa(0, 0, 0, DIRECT).start()
                yb_msg(1).start()

            @pl.when(done == 2)
            def _():
                xa(0, 1, 0, DIRECT).start()
                comb_a(0, 0)

            @pl.when(done == 3)
            def _():
                start_xa(0, 1, THROUGH)

            @pl.when(done == 4)
            def _():
                xa(0, 0, 1, DIRECT).start()

            @pl.when(done == 5)
            def _():
                xa(0, 1, 1, DIRECT).start()
                start_xa(1, 0, DIRECT)

            @pl.when(done == 6)
            def _():
                take_xa(0, 0, DIRECT)
                take_xa(0, 0, COMB)
                ya_msg(0).start()
                yb_msg(2).start()

    comb_a(0, 1)
    comb_a(1, 0)
    start_xa(1, 1, THROUGH)
    start_xa(1, 1, DIRECT)
    take_yb(0)
    for s in (0, 1):
        xb(s, THROUGH).start()

    def to_y_rep():
        return remote(bsend, by, RY, rep=rep_y)

    def to_z_rep(i):
        return remote(bsum, bz.at[i], RZ + i, rep=rep_z[i])

    load_m.wait()
    low, lowt, high = low_ref[...], lowt_ref[...], high_ref[...]
    rows_low = dot(low, m[...])
    for g in range(4):
        mband[:, 64 * g : 64 * g + 64] = momentum_decay * dot(rows_low[:, 256 * g : 256 * g + 256], lowt)

    take_yb(1)
    xb(0, DIRECT).start()
    take_xa(0, 1, DIRECT)
    take_xa(0, 1, COMB)
    take_ya(0)
    glow[...] = buf[1, OWN + 1, :LOW, :].T
    bsend[...] = mband[...] + dot(low, glow[...])
    to_y_rep().start()

    take_xa(1, 0, DIRECT)
    take_xa(1, 0, COMB)
    ya_msg(1).start()
    yb_msg(3).start()

    cleared = glow[...] - dot(lowt, bsend[...])
    for g in range(4):
        cols = slice(256 * g, 256 * g + 256)
        next_ref[:, cols] = momentum_decay * m[:, cols] + dot(cleared[:, 64 * g : 64 * g + 64], low)

    comb_a(1, 1)
    take_yb(2)
    xb(1, DIRECT).start()
    to_y_rep().wait_recv()
    bsum[...] = bsend[...] + by[...]
    for i in range(3):
        to_z_rep(i).start()
    for s in (0, 1):
        take_xb(s, THROUGH)
        xb(s, COMB).start()

    def restore(g):
        rows = slice(LOW + 192 * g, LOW + 192 * g + 192)
        cols = slice(256 * g, 256 * g + 256)
        next_ref[:, cols] = next_ref[:, cols] + dot(buf[1, OWN + 1, rows, :].T, high)

    for i in range(3):
        to_z_rep(i).wait_recv()
    bsum_all = ((bsum[...] + bz[1]) + (bz[0] + bz[2])) * 0.125
    wide = dot(lowt, bsum_all)
    for g in range(4):
        update_ref[:, 256 * g : 256 * g + 256] = dot(wide[:, 64 * g : 64 * g + 64], low)

    take_xa(1, 1, DIRECT)
    take_xa(1, 1, COMB)
    take_ya(1)
    restore(0)
    for s in (0, 1):
        take_xb(s, DIRECT)
    take_yb(3)
    for s in (0, 1):
        take_xb(s, COMB)
    for g in (1, 2, 3):
        restore(g)

    for k in range(8):
        pair(k).wait_send()
    for s in (0, 1):
        for kind in range(3):
            for p in (0, 1):
                for j in (0, 1):
                    xa(p, s, j, kind).wait_send()
            xb(s, kind).wait_send()
    for i in range(4):
        yb_msg(i).wait_send()
    for p in (0, 1):
        ya_msg(p).wait_send()
    to_y_rep().wait_send()
    for i in range(3):
        to_z_rep(i).wait_send()


def out_kernel(next_in, update_in, next_out, update_out, sem):
    copies = [pltpu.make_async_copy(src, dst, sem.at[i])
              for i, (src, dst) in enumerate(((next_in, next_out), (update_in, update_out)))]
    for copy in copies:
        copy.start()
    for copy in copies:
        copy.wait()


def vmem():
    return pl.BlockSpec(memory_space=pltpu.VMEM)


def body(activations, cotangent, momentum):
    base = basis()
    blocks = np.eye(FB // CH)
    low = np.kron(blocks, base[:BAND])
    high = np.kron(blocks, base[BAND:])
    wave = np.concatenate([low, high]).astype(np.float32)
    coarse = wave.astype(BF16)
    wave = np.stack([coarse, (wave - coarse.astype(np.float32)).astype(BF16)])
    low, high = low.astype(np.float32), high.astype(np.float32)
    any_space = pl.BlockSpec(memory_space=pl.ANY)
    nb = 4 * BAND
    whole = jax.ShapeDtypeStruct((FB, KV), F32)
    cleared, update = pl.pallas_call(
        main_kernel,
        name="step",
        out_shape=(whole, whole),
        in_specs=[any_space] * 3 + [vmem()] * 4,
        out_specs=(vmem(), vmem()),
        scratch_shapes=[
            pltpu.VMEM((TOK, D), BF16),
            pltpu.VMEM((TOK, KV), BF16),
            pltpu.VMEM((KV, TOK), BF16),
            pltpu.VMEM((FB, KV), F32),
            pltpu.VMEM((2, 8, KV, FB), F32),
            pltpu.VMEM((8, KV, FB), F32),
            pltpu.VMEM((2, 2, 3, NA[0] // 2, FB), F32),
            pltpu.VMEM((2, 2, 3, NA[1] // 2, FB), F32),
            pltpu.VMEM((2, 3, HB, FB), F32),
            pltpu.VMEM((4, NB, FB), F32),
            pltpu.VMEM((NA[0], FB), F32),
            pltpu.VMEM((NA[1], FB), F32),
            pltpu.VMEM((nb, LOW), F32),
            pltpu.VMEM((FB, LOW), F32),
            pltpu.VMEM((nb, LOW), F32),
            pltpu.VMEM((nb, LOW), F32),
            pltpu.VMEM((nb, LOW), F32),
            pltpu.VMEM((3, nb, LOW), F32),
            pltpu.SemaphoreType.DMA((NSEM,)),
            pltpu.SemaphoreType.DMA((NSEM,)),
            pltpu.SemaphoreType.DMA((2 + XCH,)),
        ],
        compiler_params=pltpu.CompilerParams(
            collective_id=0, has_side_effects=True, vmem_limit_bytes=64 * 1024 * 1024 - 256 * 1024),
    )(activations[0], cotangent[0], momentum[0], jnp.asarray(wave), jnp.asarray(low),
      jnp.asarray(np.ascontiguousarray(low.T)), jnp.asarray(high))
    cleared, update = pl.pallas_call(
        out_kernel,
        name="outputs",
        out_shape=(whole, whole),
        in_specs=[vmem(), vmem()],
        out_specs=(any_space, any_space),
        scratch_shapes=[pltpu.SemaphoreType.DMA((2,))],
    )(cleared, update)
    return cleared[None], update


def solution(mesh):
    return jax.shard_map(
        body,
        mesh=mesh,
        in_specs=(P("rep", "fsdp", None), P("rep", "fsdp", None), P("rep", "fsdp", None)),
        out_specs=(P("rep", "fsdp", None), P("fsdp", None)),
        check_vma=False,
    )
```

time: 93.7 us -> 81.1 us (0.87)
  Pallas kernels: 92.9 us -> 80 us
    pallas_call x2, Pallas kernels: 92.9 us -> 80 us  [the longest x1 77.1 us: body(): pl.pallas_call(main_kernel, name='step', out_shape=(whole, whole), in_spe...]
where the time goes in v2:
time: 81.1 us; the launch traced here: 80.6 us
  Pallas kernels  80 us (99%)
    pallas_call x1, Pallas kernels, body(): pl.pallas_call(main_kernel, name='step', out_shape=(whole, whole), in_spe...  77.1 us
    pallas_call x1, Pallas kernels, body(): pl.pallas_call(out_kernel, name='outputs', out_shape=(whole, whole), in_s...  2.87 us

profile of v2, /device:TPU:0, one launch (start us, length us, event | category | flops | bytes accessed | tf_op | source)
XLA Modules:
  0.0 80.6 jit_solution(909654205171723946)
XLA Ops:
  0.6 77.1 %step.1 = (f32[256,1024]{1,0:T(8,128)}, f32[256,1024]{1,0:T(8,128)}) custom-call(bf16[2048,4096]{1,0:T(8,128)(2,1)} %bitcast.4, bf16[2048,1024]{1,0:T(8,128)(2,1)} %bitcast.5, f32[256,1024]{1,0:T(8,128)} %bitcast.6, bf16[2,256,256]{2,1,0:T(8,128)(2,1)} %constant.8.clone.wave_ref, f32[64,256]{1,0:T(8,128)} %constant.9.clone.low_ref, ...), custom_call_target="tpu_custom_call" | custom-call | tf_op jit(solution)/shard_map/step/pallas_call | solution.py:357
  77.7 2.9 %outputs.1 = (f32[256,1024]{1,0:T(8,128)}, f32[256,1024]{1,0:T(8,128)}) custom-call(f32[256,1024]{1,0:T(8,128)} %get-tuple-element.6.next_in, f32[256,1024]{1,0:T(8,128)} %get-tuple-element.7.update_in), custom_call_target="tpu_custom_call" | custom-call | tf_op jit(solution)/shard_map/outputs/pallas_call | solution.py:390

commit v3 on v2

--- a/solution.py
+++ b/solution.py
@@ -24,7 +24,7 @@
 HB = NB // 2
 XCH = 8
 XR = TOK // XCH
-RB = 128
+RB = 64
 MESH = pl.DeviceIdType.MESH
 F32 = jnp.float32
 BF16 = jnp.bfloat16
@@ -53,9 +53,9 @@
     return jnp.dot(a, b, precision=HI, preferred_element_type=F32)
 
 
-def main_kernel(a_hbm, c_hbm, m_hbm, wave_ref, low_ref, lowt_ref, high_ref, next_ref, update_ref,
-                n, c, ct, m, buf, d2d, ral, rah, rb, yb, yal, yah, mband, glow, bsend, by, bsum, bz,
-                send_sem, recv_sem, load_sem):
+def main_kernel(a_hbm, c_hbm, m_hbm, wave_ref, low_ref, lowt_ref, high_ref, next_hbm, update_hbm,
+                next_ref, update_ref, n, c, ct, m, buf, d2d, ral, rah, rb, yb, yal, yah, mband, glow, bsend, by, bsum, bz,
+                send_sem, recv_sem, load_sem, out_sem):
     rep = lax.axis_index("rep")
     me = lax.axis_index("fsdp")
     x, y, core = me // 4, (me // 2) % 2, me % 2
@@ -293,17 +293,24 @@
         cols = slice(256 * g, 256 * g + 256)
         next_ref[:, cols] = next_ref[:, cols] + dot(buf[1, OWN + 1, rows, :].T, high)
 
+    def put(g):
+        cols = pl.ds(256 * g, 256)
+        return pltpu.make_async_copy(next_ref.at[:, cols], next_hbm.at[:, cols], out_sem.at[g])
+
+    put_update = pltpu.make_async_copy(update_ref, update_hbm, out_sem.at[4])
     for i in range(3):
         to_z_rep(i).wait_recv()
     bsum_all = ((bsum[...] + bz[1]) + (bz[0] + bz[2])) * 0.125
     wide = dot(lowt, bsum_all)
     for g in range(4):
         update_ref[:, 256 * g : 256 * g + 256] = dot(wide[:, 64 * g : 64 * g + 64], low)
+    put_update.start()
 
     take_xa(1, 1, DIRECT)
     take_xa(1, 1, COMB)
     take_ya(1)
     restore(0)
+    put(0).start()
     for s in (0, 1):
         take_xb(s, DIRECT)
     take_yb(3)
@@ -311,6 +318,10 @@
         take_xb(s, COMB)
     for g in (1, 2, 3):
         restore(g)
+        put(g).start()
+    put_update.wait()
+    for g in range(4):
+        put(g).wait()
 
     for k in range(8):
         pair(k).wait_send()
@@ -329,13 +340,23 @@
         to_z_rep(i).wait_send()
 
 
-def out_kernel(next_in, update_in, next_out, update_out, sem):
-    copies = [pltpu.make_async_copy(src, dst, sem.at[i])
-              for i, (src, dst) in enumerate(((next_in, next_out), (update_in, update_out)))]
-    for copy in copies:
-        copy.start()
-    for copy in copies:
-        copy.wait()
+def out_kernel(next_in, update_in, next_out, update_out, held, get_sem, put_sem):
+    pieces = 4
+    rows = FB // pieces
+    gets, puts = [], []
+    for i, (src, dst) in enumerate(((update_in, update_out), (next_in, next_out))):
+        for j in range(pieces):
+            at = pl.ds(j * rows, rows)
+            sem = i * pieces + j
+            gets.append(pltpu.make_async_copy(src.at[at], held.at[i, at], get_sem.at[sem]))
+            puts.append(pltpu.make_async_copy(held.at[i, at], dst.at[at], put_sem.at[sem]))
+    for get in gets:
+        get.start()
+    for get, put in zip(gets, puts):
+        get.wait()
+        put.start()
+    for put in puts:
+        put.wait()
 
 
 def vmem():
@@ -359,8 +380,10 @@
         name="step",
         out_shape=(whole, whole),
         in_specs=[any_space] * 3 + [vmem()] * 4,
-        out_specs=(vmem(), vmem()),
+        out_specs=(any_space, any_space),
         scratch_shapes=[
+            pltpu.VMEM((FB, KV), F32),
+            pltpu.VMEM((FB, KV), F32),
             pltpu.VMEM((TOK, D), BF16),
             pltpu.VMEM((TOK, KV), BF16),
             pltpu.VMEM((KV, TOK), BF16),
@@ -382,6 +405,7 @@
             pltpu.SemaphoreType.DMA((NSEM,)),
             pltpu.SemaphoreType.DMA((NSEM,)),
             pltpu.SemaphoreType.DMA((2 + XCH,)),
+            pltpu.SemaphoreType.DMA((5,)),
         ],
         compiler_params=pltpu.CompilerParams(
             collective_id=0, has_side_effects=True, vmem_limit_bytes=64 * 1024 * 1024 - 256 * 1024),
@@ -391,9 +415,13 @@
         out_kernel,
         name="outputs",
         out_shape=(whole, whole),
-        in_specs=[vmem(), vmem()],
+        in_specs=[any_space, any_space],
         out_specs=(any_space, any_space),
-        scratch_shapes=[pltpu.SemaphoreType.DMA((2,))],
+        scratch_shapes=[
+            pltpu.VMEM((2, FB, KV), F32),
+            pltpu.SemaphoreType.DMA((8,)),
+            pltpu.SemaphoreType.DMA((8,)),
+        ],
     )(cleared, update)
     return cleared[None], update
 

time: 81.1 us -> 79.6 us (0.982)
  Pallas kernels: 80 us -> 78.5 us
    pallas_call x1, Pallas kernels: 77.1 us -> 76.1 us  [body(): pl.pallas_call(main_kernel, name='step', out_shape=(whole, whole), in_spe...]
where the time goes in v3:
time: 79.6 us; the launch traced here: 79.1 us
  Pallas kernels  78.5 us (99%)
    pallas_call x1, Pallas kernels, body(): pl.pallas_call(main_kernel, name='step', out_shape=(whole, whole), in_spe...  76.1 us
    pallas_call x1, Pallas kernels, body(): pl.pallas_call(out_kernel, name='outputs', out_shape=(whole, whole), in_s...  2.4 us

profile of v3, /device:TPU:0, one launch (start us, length us, event | category | flops | bytes accessed | tf_op | source)
XLA Modules:
  0.0 79.1 jit_solution(10336214619127412173)
XLA Ops:
  0.6 76.1 %step.1 = (f32[256,1024]{1,0:T(8,128)}, f32[256,1024]{1,0:T(8,128)}) custom-call(bf16[2048,4096]{1,0:T(8,128)(2,1)} %bitcast.4, bf16[2048,1024]{1,0:T(8,128)(2,1)} %bitcast.5, f32[256,1024]{1,0:T(8,128)} %bitcast.6, bf16[2,256,256]{2,1,0:T(8,128)(2,1)} %constant.8.clone.wave_ref, f32[64,256]{1,0:T(8,128)} %constant.9.clone.low_ref, ...), custom_call_target="tpu_custom_call" | custom-call | tf_op jit(solution)/shard_map/step/pallas_call | solution.py:378
  76.7 2.4 %outputs.1 = (f32[256,1024]{1,0:T(8,128)}, f32[256,1024]{1,0:T(8,128)}) custom-call(f32[256,1024]{1,0:T(8,128)} %get-tuple-element.6.next_in, f32[256,1024]{1,0:T(8,128)} %get-tuple-element.7.update_in), custom_call_target="tpu_custom_call" | custom-call | tf_op jit(solution)/shard_map/outputs/pallas_call | solution.py:414
